TPU v7x, 64 devices: a 2x2x8 block of a 4x4x8 slice. The times are simulated.
64 devices in a mesh: dp: 4 (over x, y), tp: 16 (over z, core).
Axes of the slice: x: 2, y: 2, z: 8, core: 2. Of those that a mesh axis runs over, the one named last changes fastest.
The devices are a block of a 4x4x8 slice.
Arguments:
- x_in: bfloat16 [64, 4096], P('dp'), parts along dimension 0
- tok_pos: int32 [64], P('dp'), parts along dimension 0
- conv_state: bfloat16 [2, 64, 3, 4096], P(None, 'dp', None, 'tp'), parts along dimension 1
- lru_state: float32 [2, 64, 4096], P(None, 'dp', 'tp'), parts along dimension 1
- k_cache: bfloat16 [64, 2048, 256], P('dp'), parts along dimension 0
- v_cache: bfloat16 [64, 2048, 256], P('dp'), parts along dimension 0
- slot_pos: int32 [64, 2048], P('dp'), parts along dimension 0
- norm_scale: bfloat16 [3, 2, 4096], replicated
- rec_wx: bfloat16 [2, 4096, 4096], P(None, None, 'tp')
- rec_bx: bfloat16 [2, 4096], P(None, 'tp')
- rec_wy: bfloat16 [2, 4096, 4096], P(None, None, 'tp')
- rec_by: bfloat16 [2, 4096], P(None, 'tp')
- conv_w: bfloat16 [2, 4, 4096], P(None, None, 'tp')
- conv_b: bfloat16 [2, 4096], P(None, 'tp')
- gate_wa: bfloat16 [2, 16, 256, 256], P(None, 'tp')
- gate_ba: bfloat16 [2, 4096], P(None, 'tp')
- gate_wi: bfloat16 [2, 16, 256, 256], P(None, 'tp')
- gate_bi: bfloat16 [2, 4096], P(None, 'tp')
- a_param: float32 [2, 4096], P(None, 'tp')
- rec_wout: bfloat16 [2, 4096, 4096], P(None, 'tp')
- rec_bout: bfloat16 [2, 4096], replicated
- attn_wq: bfloat16 [4096, 4096], P(None, 'tp')
- attn_wk: bfloat16 [4096, 256], replicated
- attn_wv: bfloat16 [4096, 256], replicated
- attn_wo: bfloat16 [4096, 4096], P('tp')
- attn_bo: bfloat16 [4096], replicated
- mlp_w1: bfloat16 [3, 4096, 12288], P(None, None, 'tp')
- mlp_b1: bfloat16 [3, 12288], P(None, 'tp')
- mlp_w2: bfloat16 [3, 4096, 12288], P(None, None, 'tp')
- mlp_b2: bfloat16 [3, 12288], P(None, 'tp')
- mlp_wd: bfloat16 [3, 12288, 4096], P(None, 'tp')
- mlp_bd: bfloat16 [3, 4096], replicated
Outputs:
- output 1: bfloat16 [64, 4096], P('dp'), parts along dimension 0
- output 2: bfloat16 [2, 64, 3, 4096], P(None, 'dp', None, 'tp'), parts along dimension 1
- output 3: float32 [2, 64, 4096], P(None, 'dp', 'tp'), parts along dimension 1
- output 4: bfloat16 [64, 2048, 256], P('dp'), parts along dimension 0
- output 5: bfloat16 [64, 2048, 256], P('dp'), parts along dimension 0
- output 6: int32 [64, 2048], P('dp'), parts along dimension 0
There are 4 independent parts. A program takes and returns all parts, laid end to end along the dimension named above; an argument that names none is the same for every part.
All inputs are finite; a program needn't handle non-finite values.
Results may differ from a plain program's by a relative error of at most 0.02.
Values are sent between devices in bfloat16 or wider.
A program may use at most 768 MiB of HBM per device.

v0:
```python
import jax
import jax.numpy as jnp
from jax import lax
from jax.sharding import PartitionSpec as P

ROPE_BASE = 10000.0
NORM_EPS = 1e-6


def rms_norm(residual, scale):
    res_f = residual.astype(jnp.float32)
    mean_sq = jnp.mean(res_f * res_f, axis=-1, keepdims=True)
    return (res_f * lax.rsqrt(mean_sq + NORM_EPS) * (1.0 + scale.astype(jnp.float32))).astype(jnp.bfloat16)


def add_update(residual, update, out_bias):
    return (residual.astype(jnp.float32) + update.astype(jnp.bfloat16).astype(jnp.float32) + out_bias.astype(jnp.float32)).astype(jnp.bfloat16)


def rope_tables(tok_pos, head_dim):
    quarter = head_dim // 4
    inv_freq = ROPE_BASE ** (-jnp.arange(quarter, dtype=jnp.float32) / quarter)
    angles = tok_pos.astype(jnp.float32)[:, None] * inv_freq[None, :]
    return jnp.cos(angles), jnp.sin(angles)


def apply_rope(vectors, cosine, sine):
    quarter = vectors.shape[-1] // 4
    first = vectors[..., :quarter]
    second = vectors[..., quarter:2 * quarter]
    return jnp.concatenate([first * cosine - second * sine, second * cosine + first * sine, vectors[..., 2 * quarter:]], axis=-1)


def mlp_update(normed, w_up, b_up, w_lin, b_lin, w_down):
    gate_pre = jnp.dot(normed, w_up, preferred_element_type=jnp.float32) + b_up.astype(jnp.float32)
    lin_pre = jnp.dot(normed, w_lin, preferred_element_type=jnp.float32) + b_lin.astype(jnp.float32)
    hidden = (jax.nn.gelu(gate_pre, approximate=True) * lin_pre).astype(jnp.bfloat16)
    return jnp.dot(hidden, w_down, preferred_element_type=jnp.float32)


def recurrent_update(normed, tok_pos, conv_prev, lru_prev, rec_wx, rec_bx, rec_wy, rec_by, conv_w, conv_b, gate_wa, gate_ba, gate_wi, gate_bi, a_param, rec_wout):
    n_rows = normed.shape[0]
    n_blocks = gate_wa.shape[0]
    block_width = gate_wa.shape[1]
    x_branch = (jnp.dot(normed, rec_wx, preferred_element_type=jnp.float32) + rec_bx.astype(jnp.float32)).astype(jnp.bfloat16)
    y_branch = jax.nn.gelu(jnp.dot(normed, rec_wy, preferred_element_type=jnp.float32) + rec_by.astype(jnp.float32), approximate=True)
    tap_keep = tok_pos[:, None, None] >= jnp.arange(3, 0, -1, dtype=jnp.int32)[None, :, None]
    history = jnp.where(tap_keep, conv_prev.astype(jnp.float32), 0.0)
    tap_w = conv_w.astype(jnp.float32)
    conv_sum = conv_b.astype(jnp.float32) + tap_w[0] * x_branch.astype(jnp.float32) + jnp.sum(history * tap_w[:0:-1][None], axis=1)
    conv_x = conv_sum.astype(jnp.bfloat16)
    blocks = conv_x.reshape(n_rows, n_blocks, block_width)
    r_pre = jnp.einsum('bhi,hij->bhj', blocks, gate_wa, preferred_element_type=jnp.float32).reshape(n_rows, -1) + gate_ba.astype(jnp.float32)
    i_pre = jnp.einsum('bhi,hij->bhj', blocks, gate_wi, preferred_element_type=jnp.float32).reshape(n_rows, -1) + gate_bi.astype(jnp.float32)
    log_a = -8.0 * jax.nn.sigmoid(r_pre) * jax.nn.softplus(a_param)
    decay_gate = jnp.exp(log_a)
    in_scale = jnp.sqrt(1.0 - decay_gate * decay_gate)
    is_reset = (tok_pos == 0)[:, None]
    decay_gate = jnp.where(is_reset, 0.0, decay_gate)
    in_scale = jnp.where(is_reset, 1.0, in_scale)
    lru_new = decay_gate * lru_prev + in_scale * jax.nn.sigmoid(i_pre) * conv_x.astype(jnp.float32)
    gated_h = (lru_new * y_branch).astype(jnp.bfloat16)
    update = jnp.dot(gated_h, rec_wout, preferred_element_type=jnp.float32)
    conv_new = jnp.concatenate([conv_prev[:, 1:], x_branch[:, None, :]], axis=1)
    return update, conv_new, lru_new


def project_qkv(normed, tok_pos, attn_wq, attn_wk, attn_wv):
    n_rows = normed.shape[0]
    head_dim = attn_wk.shape[1]
    cosine, sine = rope_tables(tok_pos, head_dim)
    q_heads = jnp.dot(normed, attn_wq, preferred_element_type=jnp.float32).reshape(n_rows, -1, head_dim)
    q_heads = apply_rope(q_heads, cosine[:, None, :], sine[:, None, :]).astype(jnp.bfloat16)
    k_new = apply_rope(jnp.dot(normed, attn_wk, preferred_element_type=jnp.float32), cosine, sine).astype(jnp.bfloat16)
    v_new = jnp.dot(normed, attn_wv, preferred_element_type=jnp.float32).astype(jnp.bfloat16)
    return q_heads, k_new, v_new


def write_cache(tok_pos, k_new, v_new, k_cache, v_cache, slot_pos):
    window = k_cache.shape[1]
    target = jnp.arange(window, dtype=jnp.int32)[None, :] == (tok_pos % window)[:, None]
    k_next = jnp.where(target[:, :, None], k_new[:, None, :], k_cache)
    v_next = jnp.where(target[:, :, None], v_new[:, None, :], v_cache)
    slot_next = jnp.where(target, tok_pos[:, None], slot_pos)
    return k_next, v_next, slot_next


def attend(q_heads, tok_pos, k_next, v_next, slot_next, attn_wo):
    n_rows = q_heads.shape[0]
    window = k_next.shape[1]
    head_dim = k_next.shape[2]
    slot_age = tok_pos[:, None] - slot_next
    slot_valid = (slot_next >= 0) & (slot_age >= 0) & (slot_age < window)
    scores = jnp.einsum('bhd,bsd->bhs', q_heads, k_next, preferred_element_type=jnp.float32) * (head_dim ** -0.5)
    scores = jnp.where(slot_valid[:, None, :], scores, -jnp.inf)
    probs_bf = jax.nn.softmax(scores, axis=-1).astype(jnp.bfloat16)
    heads_out = jnp.einsum('bhs,bsd->bhd', probs_bf, v_next, preferred_element_type=jnp.float32).astype(jnp.bfloat16)
    return jnp.dot(heads_out.reshape(n_rows, -1), attn_wo, preferred_element_type=jnp.float32)


def io_specs():
    in_specs = (P('dp', None), P('dp'), P(None, 'dp', None, 'tp'), P(None, 'dp', 'tp'), P('dp', None, None), P('dp', None, None), P('dp', None),
                P(), P(None, None, 'tp'), P(None, 'tp'), P(None, None, 'tp'), P(None, 'tp'), P(None, None, 'tp'), P(None, 'tp'),
                P(None, 'tp', None, None), P(None, 'tp'), P(None, 'tp', None, None), P(None, 'tp'), P(None, 'tp'), P(None, 'tp', None), P(),
                P(None, 'tp'), P(), P(), P('tp', None), P(),
                P(None, None, 'tp'), P(None, 'tp'), P(None, None, 'tp'), P(None, 'tp'), P(None, 'tp', None), P())
    out_specs = (P('dp', None), P(None, 'dp', None, 'tp'), P(None, 'dp', 'tp'), P('dp', None, None), P('dp', None, None), P('dp', None))
    return in_specs, out_specs


def solution(mesh):
    in_specs, out_specs = io_specs()

    def local_step(x_in, tok_pos, conv_state, lru_state, k_cache, v_cache, slot_pos, norm_scale, rec_wx, rec_bx, rec_wy, rec_by, conv_w, conv_b, gate_wa, gate_ba, gate_wi, gate_bi, a_param, rec_wout, rec_bout, attn_wq, attn_wk, attn_wv, attn_wo, attn_bo, mlp_w1, mlp_b1, mlp_w2, mlp_b2, mlp_wd, mlp_bd):
        residual = x_in
        conv_list = []
        lru_list = []
        for layer_idx in range(3):
            normed = rms_norm(residual, norm_scale[layer_idx, 0])
            if layer_idx < 2:
                part_sum, conv_new, lru_new = recurrent_update(normed, tok_pos, conv_state[layer_idx], lru_state[layer_idx], rec_wx[layer_idx], rec_bx[layer_idx], rec_wy[layer_idx], rec_by[layer_idx], conv_w[layer_idx], conv_b[layer_idx], gate_wa[layer_idx], gate_ba[layer_idx], gate_wi[layer_idx], gate_bi[layer_idx], a_param[layer_idx], rec_wout[layer_idx])
                conv_list.append(conv_new)
                lru_list.append(lru_new)
                out_bias = rec_bout[layer_idx]
            else:
                q_heads, k_new, v_new = project_qkv(normed, tok_pos, attn_wq, attn_wk, attn_wv)
                k_next, v_next, slot_next = write_cache(tok_pos, k_new, v_new, k_cache, v_cache, slot_pos)
                part_sum = attend(q_heads, tok_pos, k_next, v_next, slot_next, attn_wo)
                out_bias = attn_bo
            residual = add_update(residual, lax.psum(part_sum.astype(jnp.bfloat16), 'tp'), out_bias)
            normed = rms_norm(residual, norm_scale[layer_idx, 1])
            part_sum = mlp_update(normed, mlp_w1[layer_idx], mlp_b1[layer_idx], mlp_w2[layer_idx], mlp_b2[layer_idx], mlp_wd[layer_idx])
            residual = add_update(residual, lax.psum(part_sum.astype(jnp.bfloat16), 'tp'), mlp_bd[layer_idx])
        return (residual, jnp.stack(conv_list), jnp.stack(lru_list), k_next, v_next, slot_next)

    return jax.shard_map(local_step, mesh=mesh, in_specs=in_specs, out_specs=out_specs, check_vma=False)
```

profile of v0, /device:TPU:21, one launch (start us, length us, event | category | flops | bytes accessed | tf_op | source)
XLA Modules:
  0.0 763.8 jit_solution(18430863215198138510)
XLA Ops:
  12.2 1.0 fusion.138
  17.2 2.1 add_convert_fusion.1
  19.3 1.1 fusion.125
  20.3 1.1 fusion.119
  21.4 4.3 convolution_convert_fusion.2
  26.2 107.4 %all-reduce.7.cloned.1.call-done = bf16[16,4096]{1,0:T(8,128)(2,1)} async-done(((bf16[16,4096]{1,0:T(8,128)(2,1)}), bf16[16,4096]{1,0:T(8,128)(2,1)}) %all-reduce.7.cloned.1.call-update) | async-done | bytes 131088 | tf_op jit(solution)/shard_map/psum | solution.py:130
  133.6 1.1 fusion.143
  134.7 3.8 fusion.187
  138.5 7.8 %fusion.27 = bf16[16,4096]{1,0:T(8,128)(2,1)} fusion(bf16[3,768,4096]{2,1,0:T(8,128)(2,1)} %param.62, f32[16,768]{1,0:T(8,128)S(1)} %fusion.187, bf16[3,4096,768]{2,1,0:T(8,128)(2,1)} %param.60, bf16[16,4096]{1,0:T(8,128)(2,1)S(1)} %get-tuple-element.26, f32[4096]{0:T(1024)S(1)} %bitcast.224, f32[16]{0:T(128)S(1)} %add_rsqrt_fusion.4, ...), kind=kOutput, calls=%fused_computation.29 | convolution fusion | flops 201691136 | bytes 12913728 | tf_op jit(solution)/shard_map/dot_general | solution.py:38
  146.4 103.8 %all-reduce.9.cloned.1.call-done = bf16[16,4096]{1,0:T(8,128)(2,1)} async-done(((bf16[16,4096]{1,0:T(8,128)(2,1)}), bf16[16,4096]{1,0:T(8,128)(2,1)}) %all-reduce.9.cloned.1.call-update) | async-done | bytes 131088 | tf_op jit(solution)/shard_map/psum | solution.py:133
  250.2 1.1 fusion.148
  251.2 2.0 add_convert_fusion
  253.6 4.2 convolution_convert_fusion.1
  258.0 103.8 %all-reduce.11.cloned.1.call-done = bf16[16,4096]{1,0:T(8,128)(2,1)} async-done(((bf16[16,4096]{1,0:T(8,128)(2,1)}), bf16[16,4096]{1,0:T(8,128)(2,1)}) %all-reduce.11.cloned.1.call-update) | async-done | bytes 131088 | tf_op jit(solution)/shard_map/psum | solution.py:130
  361.8 1.1 fusion.153
  362.9 3.8 fusion.196
  366.7 7.7 %fusion.30 = bf16[16,4096]{1,0:T(8,128)(2,1)} fusion(bf16[3,768,4096]{2,1,0:T(8,128)(2,1)} %param.62, f32[16,768]{1,0:T(8,128)S(1)} %fusion.196, bf16[3,4096,768]{2,1,0:T(8,128)(2,1)} %param.60, bf16[16,4096]{1,0:T(8,128)(2,1)S(1)} %get-tuple-element.22, f32[4096]{0:T(1024)S(1)} %bitcast.220, f32[16]{0:T(128)S(1)} %add_rsqrt_fusion.2, ...), kind=kOutput, calls=%fused_computation.30 | convolution fusion | flops 201691136 | bytes 12913728 | tf_op jit(solution)/shard_map/dot_general | solution.py:38
  374.7 103.6 %all-reduce.13.cloned.1.call-done = bf16[16,4096]{1,0:T(8,128)(2,1)} async-done(((bf16[16,4096]{1,0:T(8,128)(2,1)}), bf16[16,4096]{1,0:T(8,128)(2,1)}) %all-reduce.13.cloned.1.call-update) | async-done | bytes 131088 | tf_op jit(solution)/shard_map/psum | solution.py:133
  478.3 1.1 fusion.158
  479.4 2.0 fusion.317
  481.4 2.0 convolution_bitcast_fusion
  483.7 2.0 convolution_convert_fusion.3
  485.8 28.5 %broadcast_select_fusion.1 = (bf16[16,2048,256]{2,1,0:T(8,128)(2,1)}, bf16[16,2048,256]{2,1,0:T(8,128)(2,1)}) fusion(bf16[16,2048,256]{2,1,0:T(8,128)(2,1)} %param.36, pred[16,2048]{1,0:T(8,128)(4,1)S(1)} %iota_compare_fusion, bf16[16,256]{1,0:T(8,128)(2,1)S(1)} %pad_maximum_fusion.2, bf16[16,2048,256]{2,1,0:T(8,128)(2,1)} %param.37, ...), kind=kLoop, calls=%fused_computation.1 | loop fusion | flops 16777216 | bytes 67158016 | tf_op jit(solution)/shard_map/jit(_where)/select_n | solution.py:82
  514.4 10.2 %fusion.274 = f32[16,1,2048]{2,1,0:T(1,128)S(1)} fusion(bf16[16,2048,256]{2,1,0:T(8,128)(2,1)} %get-tuple-element.38, bf16[16,256,1]{1,0,2:T(8,128)(2,1)S(1)} %maximum_bitcast_fusion.2), kind=kOutput, calls=%fused_computation.225 | convolution fusion | flops 16777216 | bytes 16916480 | tf_op jit(solution)/shard_map/bhd,bsd->bhs/dot_general | solution.py:94
  525.8 8.0 %fusion.173 = bf16[16,1,256]{2,1,0:T(2,128)(2,1)S(1)} fusion(bf16[16,2048,256]{2,1,0:T(8,128)(2,1)} %get-tuple-element.39, bf16[16,2048,1]{1,0,2:T(8,128)(2,1)S(1)} %fusion.180), kind=kOutput, calls=%fused_computation.155 | convolution fusion | flops 16777216 | bytes 16850944 | tf_op jit(solution)/shard_map/bhs,bsd->bhd/dot_general | solution.py:97
  533.8 1.1 convolution_convert_fusion
  535.7 103.2 %all-reduce.15.cloned.1.call-done = bf16[16,4096]{1,0:T(8,128)(2,1)} async-done(((bf16[16,4096]{1,0:T(8,128)(2,1)}), bf16[16,4096]{1,0:T(8,128)(2,1)}) %all-reduce.15.cloned.1.call-update) | async-done | bytes 131088 | tf_op jit(solution)/shard_map/psum | solution.py:130
  638.8 1.1 fusion.163
  639.9 3.8 fusion.205
  643.7 7.7 %fusion.33 = bf16[16,4096]{1,0:T(8,128)(2,1)} fusion(bf16[3,768,4096]{2,1,0:T(8,128)(2,1)} %param.62, f32[16,768]{1,0:T(8,128)S(1)} %fusion.205, bf16[3,4096,768]{2,1,0:T(8,128)(2,1)} %param.60, bf16[16,4096]{1,0:T(8,128)(2,1)S(1)} %get-tuple-element.15, f32[4096]{0:T(1024)S(1)} %bitcast.218, f32[16]{0:T(128)S(1)} %add_rsqrt_fusion, ...), kind=kOutput, calls=%fused_computation.31 | convolution fusion | flops 201691136 | bytes 12913728 | tf_op jit(solution)/shard_map/dot_general | solution.py:38
  652.1 103.2 %all-reduce.17.cloned.1.call-done = bf16[16,4096]{1,0:T(8,128)(2,1)} async-done(((bf16[16,4096]{1,0:T(8,128)(2,1)}), bf16[16,4096]{1,0:T(8,128)(2,1)}) %all-reduce.17.cloned.1.call-update) | async-done | bytes 131088 | tf_op jit(solution)/shard_map/psum | solution.py:133
  755.3 1.6 fusion.167
  (87 shorter events, 13.2 us)
Async XLA Ops:
  7.2 526.7 %copy-start = (bf16[256,4096]{1,0:T(8,128)(2,1)S(1)}, bf16[256,4096]{1,0:T(8,128)(2,1)}, u32[]{:S(2)}) copy-start(bf16[256,4096]{1,0:T(8,128)(2,1)} %param.56) | copy-start | bytes 6291460
  7.2 18.6 %copy-start.9 = (s32[16]{0:T(128)S(1)}, s32[16]{0:T(128)}, u32[]{:S(2)}) copy-start(s32[16]{0:T(128)} %param.33) | copy-start | bytes 196
  7.2 126.4 %copy-start.1 = (bf16[16,4096]{1,0:T(8,128)(2,1)S(1)}, bf16[16,4096]{1,0:T(8,128)(2,1)}, u32[]{:S(2)}) copy-start(bf16[16,4096]{1,0:T(8,128)(2,1)} %param.32) | copy-start | bytes 393220
  7.2 18.6 %copy-start.2 = (bf16[2,16,3,256]{3,1,2,0:T(8,128)(2,1)S(1)}, bf16[2,16,3,256]{3,1,2,0:T(8,128)(2,1)}, u32[]{:S(2)}) copy-start(bf16[2,16,3,256]{3,1,2,0:T(8,128)(2,1)} %param.34) | copy-start | bytes 147460
  7.2 18.6 %copy-start.5 = (bf16[2,4096]{1,0:T(2,128)(2,1)S(1)}, bf16[2,4096]{1,0:T(2,128)(2,1)}, u32[]{:S(2)}) copy-start(bf16[2,4096]{1,0:T(2,128)(2,1)} %param.52) | copy-start | bytes 49156
  7.2 18.7 %copy-start.6 = (bf16[3,768]{1,0:T(4,128)(2,1)S(1)}, bf16[3,768]{1,0:T(4,128)(2,1)}, u32[]{:S(2)}) copy-start(bf16[3,768]{1,0:T(4,128)(2,1)} %param.59) | copy-start | bytes 13828
  7.3 18.7 %copy-start.4 = (bf16[3,4096]{1,0:T(4,128)(2,1)S(1)}, bf16[3,4096]{1,0:T(4,128)(2,1)}, u32[]{:S(2)}) copy-start(bf16[3,4096]{1,0:T(4,128)(2,1)} %param.63) | copy-start | bytes 73732
  7.3 18.8 %copy-start.8 = (bf16[4096]{0:T(1024)(128)(2,1)S(1)}, bf16[4096]{0:T(1024)(128)(2,1)}, u32[]{:S(2)}) copy-start(bf16[4096]{0:T(1024)(128)(2,1)} %param.57) | copy-start | bytes 24580
  7.3 18.9 %copy-start.7 = (bf16[3,768]{1,0:T(4,128)(2,1)S(1)}, bf16[3,768]{1,0:T(4,128)(2,1)}, u32[]{:S(2)}) copy-start(bf16[3,768]{1,0:T(4,128)(2,1)} %param.61) | copy-start | bytes 13828
  7.3 126.3 %all-reduce.7.cloned.1.call-start = ((), (), s32[]{:S(2)}) async-start(), calls=%async_computation | async-start | bytes 262144 | tf_op jit(solution)/shard_map/psum | solution.py:130
  25.7 224.4 %all-reduce.9.cloned.1.call-start = ((), (), s32[]{:S(2)}) async-start(), calls=%async_computation.1 | async-start | bytes 262144 | tf_op jit(solution)/shard_map/psum | solution.py:133
  138.4 114.8 %copy-start.10 = (bf16[2,1,256,256]{3,2,1,0:T(8,128)(2,1)S(1)}, bf16[2,1,256,256]{3,2,1,0:T(8,128)(2,1)}, u32[]{:S(2)}) copy-start(bf16[2,1,256,256]{3,2,1,0:T(8,128)(2,1)} %param.46) | copy-start | bytes 786436
  138.5 115.0 %copy-start.11 = (bf16[2,1,256,256]{3,2,1,0:T(8,128)(2,1)S(1)}, bf16[2,1,256,256]{3,2,1,0:T(8,128)(2,1)}, u32[]{:S(2)}) copy-start(bf16[2,1,256,256]{3,2,1,0:T(8,128)(2,1)} %param.48) | copy-start | bytes 786436
  138.5 115.0 %copy-start.12 = (f32[2,16,256]{2,1,0:T(8,128)S(1)}, f32[2,16,256]{2,1,0:T(8,128)}, u32[]{:S(2)}) copy-start(f32[2,16,256]{2,1,0:T(8,128)} %param.35) | copy-start | bytes 98308
  146.3 215.5 %all-reduce.11.cloned.1.call-start = ((), (), s32[]{:S(2)}) async-start(), calls=%async_computation.2 | async-start | bytes 262144 | tf_op jit(solution)/shard_map/psum | solution.py:130
  257.9 220.4 %all-reduce.13.cloned.1.call-start = ((), (), s32[]{:S(2)}) async-start(), calls=%async_computation.3 | async-start | bytes 262144 | tf_op jit(solution)/shard_map/psum | solution.py:133
  374.4 264.4 %all-reduce.15.cloned.1.call-start = ((), (), s32[]{:S(2)}) async-start(), calls=%async_computation.4 | async-start | bytes 262144 | tf_op jit(solution)/shard_map/psum | solution.py:130
  514.4 10.2 %copy-start.3 = (s32[16,2048]{1,0:T(8,128)S(1)}, s32[16,2048]{1,0:T(8,128)}, u32[]{:S(2)}) copy-start(s32[16,2048]{1,0:T(8,128)} %param.38) | copy-start | bytes 393220
  535.0 220.4 %all-reduce.17.cloned.1.call-start = ((), (), s32[]{:S(2)}) async-start(), calls=%async_computation.5 | async-start | bytes 262144 | tf_op jit(solution)/shard_map/psum | solution.py:133
Sparse Core Ops, SparseCore 0:
  25.9 107.6 all-reduce.6
  146.4 103.7 all-reduce.8
  258.0 103.7 all-reduce.10
  374.5 103.7 all-reduce.12
  535.1 103.7 all-reduce.14
  651.6 103.7 all-reduce.16
where the time goes:
time: 765 us; the launch traced here: 764 us
  waiting for transfers between devices  625 us (82%)
  matrix products  74.9 us (10%)
  other arithmetic  48.2 us (6%)
  between operations  14.5 us (2%)
    psum x6, waiting for transfers between devices, local_step(): lax.psum(part_sum.astype(jnp.bfloat16), 'tp')  625 us
    select_n x1, other arithmetic, write_cache(): k_next = jnp.where(target[:, :, None], k_new[:, None, :], k_cache)  28.5 us
    dot_general x3, matrix products, mlp_update(): return jnp.dot(hidden, w_down, preferred_element_type=jnp.float32)  23.2 us
  transfers between devices with their start and end apart: 6, of which 6 were waited for; matrix products, arithmetic and copies ran while one was open for 0% of the time, Pallas kernels for 0%

commit v1 on v0

v1 whole, which is shorter than its diff:
```python
import functools

import jax
import jax.numpy as jnp
import numpy as np
from jax import lax
from jax.experimental import pallas as pl
from jax.experimental.pallas import tpu as pltpu
from jax.sharding import PartitionSpec as P

ROPE_BASE = 10000.0
NORM_EPS = 1e-6
F32 = jnp.float32
BF16 = jnp.bfloat16
MESH_ID = pl.DeviceIdType.MESH
VMEM_LIMIT = 67043328
ANY = pl.BlockSpec(memory_space=pl.ANY)
SMEM = pl.BlockSpec(memory_space=pltpu.SMEM)
VMEM = pl.BlockSpec(memory_space=pltpu.VMEM)


def gelu(x):
    return jax.nn.gelu(x, approximate=True)


def softplus(x):
    return jnp.maximum(x, 0.0) + jnp.log1p(jnp.exp(-jnp.abs(x)))


def lane_positions(pos_ref, width):
    rows = pos_ref.shape[0]
    row_ids = lax.broadcasted_iota(jnp.int32, (rows, width), 0)
    out = jnp.zeros((rows, width), jnp.int32)
    for b in range(rows):
        out = jnp.where(row_ids == b, pos_ref[b], out)
    return out


class Group:
    def __init__(self, n, sendb, rsb, res, ssem, rsem):
        self.n, self.sendb, self.rsb, self.res, self.ssem, self.rsem = n, sendb, rsb, res, ssem, rsem
        self.me = lax.axis_index("tp")
        self.chunk = res.shape[2]
        self.order = sorted(range(1, n), key=lambda k: -min(k, n - k))
        self.rs_open, self.ag_open = [], []

    def peer(self, k):
        return lax.rem(self.me + k, self.n)

    def greet(self):
        barrier = pltpu.get_barrier_semaphore()
        for k in range(1, self.n):
            pl.semaphore_signal(barrier, inc=1, device_id={"tp": self.peer(k)}, device_id_type=MESH_ID)

    def wait_greet(self):
        pl.semaphore_wait(pltpu.get_barrier_semaphore(), self.n - 1)

    def cols(self, d):
        return pl.ds(pl.multiple_of(d * self.chunk, self.chunk), self.chunk)

    def norm(self, scale_ref, layer, which, nb):
        chunk = self.chunk
        total = None
        for c in range(self.n):
            x = self.res[c].astype(F32)
            total = x * x if total is None else total + x * x
        inv = lax.rsqrt(jnp.sum(total, axis=1, keepdims=True) / (self.n * chunk) + NORM_EPS)
        for c in range(self.n):
            lanes = slice(c * chunk, (c + 1) * chunk)
            scale = 1.0 + scale_ref[layer, which:which + 1, lanes].astype(F32)
            nb[:, lanes] = (self.res[c].astype(F32) * inv * scale).astype(BF16)

    def scatter(self, h, w_ref):
        for copy in self.rs_open:
            copy.wait_send()
        self.rs_open = []
        late = None
        for k in self.order + [0]:
            dst = self.peer(k) if k else self.me
            part = jnp.dot(h, w_ref[:, self.cols(dst)], preferred_element_type=F32)
            if late is not None:
                late.start()
            if k:
                self.sendb[k] = part.astype(BF16)
                late = pltpu.make_async_remote_copy(
                    src_ref=self.sendb.at[k], dst_ref=self.rsb.at[k], send_sem=self.ssem.at[0, k], recv_sem=self.rsem.at[0, k],
                    device_id={"tp": dst}, device_id_type=MESH_ID)
                self.rs_open.append(late)
            else:
                late = None
        return part

    def finish(self, own, bias_row):
        for copy in self.rs_open:
            copy.wait_recv()
        for k in self.order:
            own = own + self.rsb[k].astype(F32)
        update = own.astype(BF16).astype(F32)
        fresh = (self.res[self.me].astype(F32) + update + bias_row.astype(F32)).astype(BF16)
        for copy in self.ag_open:
            copy.wait_send()
        self.ag_open = []
        self.res[self.me] = fresh
        for k in self.order:
            copy = pltpu.make_async_remote_copy(
                src_ref=self.res.at[self.me], dst_ref=self.res.at[self.me], send_sem=self.ssem.at[1, k], recv_sem=self.rsem.at[1, k],
                device_id={"tp": self.peer(k)}, device_id_type=MESH_ID)
            copy.start()
            self.ag_open.append(copy)
        for copy in self.ag_open:
            copy.wait_recv()
        return fresh

    def close(self):
        for copy in self.rs_open + self.ag_open:
            copy.wait_send()


def mlp(group, layer, nb, hb, w1, w2, wd, b1, b2, bd, waits):
    step = 256
    waits[0].wait()
    waits[1].wait()
    n = nb[...]
    for j in range(hb.shape[1] // step):
        lanes = slice(j * step, (j + 1) * step)
        gate = jnp.dot(n, w1[:, lanes], preferred_element_type=F32) + b1[layer:layer + 1, lanes].astype(F32)
        lin = jnp.dot(n, w2[:, lanes], preferred_element_type=F32) + b2[layer:layer + 1, lanes].astype(F32)
        hb[:, lanes] = (gelu(gate) * lin).astype(BF16)
    waits[2].wait()
    own = group.scatter(hb[...], wd)
    return group.finish(own, bd[layer:layer + 1, group.cols(group.me)])


FIRST_SMALL = ("x", "nscale", "conv", "lru", "bx", "by", "cw", "cb", "ba", "bi", "ap", "wa", "wi", "bout", "b1", "b2", "bd", "invf")
FIRST_BIG = ("wx", "wy", "wout", "w1", "w2", "wd", "wq", "wk", "wv")


def first_kernel(n, layers, pos_ref, *refs):
    names = FIRST_SMALL + FIRST_BIG
    hbm = dict(zip(names, refs))
    refs = refs[len(names):]
    xown_ref, q_ref, kn_ref, vn_ref, convo_ref, lruo_ref = refs[:6]
    refs = refs[6:]
    small = dict(zip(FIRST_SMALL, refs))
    refs = refs[len(FIRST_SMALL):]
    wxs, wys, wos, w1s, w2s, wds, qkv, nb, hb, sendb, rsb, res, ssem, rsem, lsem, bsem = refs

    group = Group(n, sendb, rsb, res, ssem, rsem)
    group.greet()

    def start(src, dst, sem, priority=0):
        copy = pltpu.make_async_copy(src, dst, sem)
        copy.start(priority=priority)
        return copy

    loads = {name: start(hbm[name], small[name], lsem.at[i]) for i, name in enumerate(FIRST_SMALL)}
    big = {}
    count = 0
    for l in range(layers):
        for name, dst in (("wx", wxs), ("wy", wys), ("wout", wos), ("w1", w1s), ("w2", w2s), ("wd", wds)):
            big[name, l] = start(hbm[name].at[l], dst.at[l], bsem.at[count], 1)
            count += 1
    for i, name in enumerate(("wq", "wk", "wv")):
        big[name] = start(hbm[name], qkv.at[i], bsem.at[count], 1)
        count += 1

    for copy in loads.values():
        copy.wait()
    chunk = res.shape[2]
    for c in range(n):
        res[c] = small["x"][:, c * chunk:(c + 1) * chunk]
    pos = lane_positions(pos_ref, chunk)

    def row(name, l):
        return small[name][l:l + 1, :].astype(F32)

    for l in range(layers):
        group.norm(small["nscale"], l, 0, nb)
        big["wx", l].wait()
        xb = (jnp.dot(nb[...], wxs[l], preferred_element_type=F32) + row("bx", l)).astype(BF16)
        big["wy", l].wait()
        y = gelu(jnp.dot(nb[...], wys[l], preferred_element_type=F32) + row("by", l))
        taps = [small["cw"][l, j:j + 1, :].astype(F32) for j in range(4)]
        old = small["conv"][l].astype(F32)
        hist = None
        for j in range(3):
            term = jnp.where(pos >= 3 - j, old[:, j, :], 0.0) * taps[3 - j]
            hist = term if hist is None else hist + term
        xc = (row("cb", l) + taps[0] * xb.astype(F32) + hist).astype(BF16)
        r_pre = jnp.dot(xc, small["wa"][l, 0], preferred_element_type=F32) + row("ba", l)
        i_pre = jnp.dot(xc, small["wi"][l, 0], preferred_element_type=F32) + row("bi", l)
        decay = jnp.exp(-8.0 * jax.nn.sigmoid(r_pre) * softplus(small["ap"][l:l + 1, :]))
        in_scale = jnp.sqrt(1.0 - decay * decay)
        decay = jnp.where(pos == 0, 0.0, decay)
        in_scale = jnp.where(pos == 0, 1.0, in_scale)
        h = decay * small["lru"][l] + in_scale * jax.nn.sigmoid(i_pre) * xc.astype(F32)
        big["wout", l].wait()
        if l == 0:
            group.wait_greet()
        own = group.scatter((h * y).astype(BF16), wos.at[l])
        lruo_ref[l] = h
        convo_ref[l] = jnp.stack([old[:, 1, :], old[:, 2, :], xb.astype(F32)], axis=1).astype(BF16)
        group.finish(own, small["bout"][l:l + 1, group.cols(group.me)])

        group.norm(small["nscale"], l, 1, nb)
        fresh = mlp(group, l, nb, hb, w1s.at[l], w2s.at[l], wds.at[l], small["b1"], small["b2"], small["bd"],
                    (big["w1", l], big["w2", l], big["wd", l]))

    xown_ref[...] = fresh
    group.norm(small["nscale"], layers, 0, nb)
    half = small["invf"].shape[1]
    angles = pos[:, :half].astype(F32) * small["invf"][...]
    cosine, sine = jnp.cos(angles), jnp.sin(angles)
    lane = lax.broadcasted_iota(jnp.int32, sine.shape, 1)
    sine = jnp.where(lane < half // 2, -sine, sine)

    def rope(v):
        turned = v[:, :half]
        return jnp.concatenate([turned * cosine + pltpu.roll(turned, half // 2, 1) * sine, v[:, half:]], axis=1)

    big["wq"].wait()
    q_ref[...] = rope(jnp.dot(nb[...], qkv[0], preferred_element_type=F32)).astype(BF16)
    big["wk"].wait()
    kn_ref[...] = rope(jnp.dot(nb[...], qkv[1], preferred_element_type=F32)).astype(BF16)
    big["wv"].wait()
    vn_ref[...] = jnp.dot(nb[...], qkv[2], preferred_element_type=F32).astype(BF16)
    group.close()


def attend_kernel(pos_ref, q_ref, kn_ref, vn_ref, conv_ref, lru_ref, slot_ref, k_hbm, v_hbm,
                  o_ref, convo_ref, lruo_ref, sloto_ref, ko_hbm, vo_hbm, kb, vb, bias, sems):
    rows, window, dim = k_hbm.shape
    loads, stores = [], []
    for b in range(rows):
        pair = []
        for i, (src, dst) in enumerate(((k_hbm, kb), (v_hbm, vb))):
            copy = pltpu.make_async_copy(src.at[b], dst.at[b], sems.at[0, i, b])
            copy.start()
            pair.append(copy)
        loads.append(pair)
    convo_ref[...] = conv_ref[...]
    lruo_ref[...] = lru_ref[...]
    pos = lane_positions(pos_ref, window)
    lane = lax.broadcasted_iota(jnp.int32, pos.shape, 1)
    slots = jnp.where(lane == lax.rem(pos, window), pos, slot_ref[...])
    sloto_ref[...] = slots
    age = pos - slots
    bias[...] = jnp.where((slots >= 0) & (age >= 0) & (age < window), 0.0, -jnp.inf)
    pack = 16
    sub = lax.broadcasted_iota(jnp.int32, (pack, dim), 0)
    for b in range(rows):
        slot = lax.rem(pos_ref[b], window)
        base = pl.multiple_of(slot // pack * pack, pack)
        for i, (buf, new) in enumerate(((kb, kn_ref), (vb, vn_ref))):
            loads[b][i].wait()
            tile = buf[b, pl.ds(base, pack), :]
            buf[b, pl.ds(base, pack), :] = jnp.where(sub == slot - base, new[b:b + 1, :].astype(F32), tile.astype(F32)).astype(BF16)
        scores = lax.dot_general(q_ref[b:b + 1, :], kb[b], (((1,), (1,)), ((), ())), preferred_element_type=F32)
        for i, (buf, dst) in enumerate(((kb, ko_hbm), (vb, vo_hbm))):
            copy = pltpu.make_async_copy(buf.at[b], dst.at[b], sems.at[1, i, b])
            copy.start()
            stores.append(copy)
        scores = scores * (dim ** -0.5) + bias[b:b + 1, :]
        weight = jnp.exp(scores - jnp.max(scores, axis=1, keepdims=True))
        probs = (weight / jnp.sum(weight, axis=1, keepdims=True)).astype(BF16)
        o_ref[b:b + 1, :] = jnp.dot(probs, vb[b], preferred_element_type=F32).astype(BF16)
    for copy in stores:
        copy.wait()


LAST_SMALL = ("o", "xown", "nscale", "bo", "b1", "b2", "bd")
LAST_BIG = ("wo", "w1", "w2", "wd")


def last_kernel(n, layer, *refs):
    names = LAST_SMALL + LAST_BIG
    hbm = dict(zip(names, refs))
    refs = refs[len(names):]
    x_ref = refs[0]
    refs = refs[1:]
    small = dict(zip(LAST_SMALL, refs))
    refs = refs[len(LAST_SMALL):]
    wos, w1s, w2s, wds, nb, hb, sendb, rsb, res, ssem, rsem, lsem, bsem = refs
    group = Group(n, sendb, rsb, res, ssem, rsem)
    group.greet()

    def start(src, dst, sem, priority=0):
        copy = pltpu.make_async_copy(src, dst, sem)
        copy.start(priority=priority)
        return copy

    loads = [start(hbm[name], small[name], lsem.at[i]) for i, name in enumerate(LAST_SMALL)]
    big = [start(hbm["wo"], wos, bsem.at[0], 1)]
    for i, (name, dst) in enumerate((("w1", w1s), ("w2", w2s), ("wd", wds))):
        big.append(start(hbm[name].at[layer], dst, bsem.at[i + 1], 1))
    for copy in loads:
        copy.wait()
    res[group.me] = small["xown"][...]
    big[0].wait()
    group.wait_greet()
    own = group.scatter(small["o"][...], wos)
    group.finish(own, small["bo"][:, group.cols(group.me)])
    group.norm(small["nscale"], layer, 1, nb)
    mlp(group, layer, nb, hb, w1s, w2s, wds, small["b1"], small["b2"], small["bd"], big[1:])
    chunk = res.shape[2]
    for c in range(n):
        x_ref[:, c * chunk:(c + 1) * chunk] = res[c]
    group.close()


def io_specs():
    in_specs = (P('dp', None), P('dp'), P(None, 'dp', None, 'tp'), P(None, 'dp', 'tp'), P('dp', None, None), P('dp', None, None), P('dp', None),
                P(), P(None, None, 'tp'), P(None, 'tp'), P(None, None, 'tp'), P(None, 'tp'), P(None, None, 'tp'), P(None, 'tp'),
                P(None, 'tp', None, None), P(None, 'tp'), P(None, 'tp', None, None), P(None, 'tp'), P(None, 'tp'), P(None, 'tp', None), P(),
                P(None, 'tp'), P(), P(), P('tp', None), P(),
                P(None, None, 'tp'), P(None, 'tp'), P(None, None, 'tp'), P(None, 'tp'), P(None, 'tp', None), P())
    out_specs = (P('dp', None), P(None, 'dp', None, 'tp'), P(None, 'dp', 'tp'), P('dp', None, None), P('dp', None, None), P('dp', None))
    return in_specs, out_specs


def vmem_like(array):
    return pltpu.VMEM(array.shape, array.dtype)


def solution(mesh):
    in_specs, out_specs = io_specs()
    n = mesh.shape["tp"]

    def local_step(x_in, tok_pos, conv_state, lru_state, k_cache, v_cache, slot_pos, norm_scale, rec_wx, rec_bx, rec_wy, rec_by, conv_w, conv_b, gate_wa, gate_ba, gate_wi, gate_bi, a_param, rec_wout, rec_bout, attn_wq, attn_wk, attn_wv, attn_wo, attn_bo, mlp_w1, mlp_b1, mlp_w2, mlp_b2, mlp_wd, mlp_bd):
        rows, width = x_in.shape
        layers, _, own = rec_wx.shape
        hidden = mlp_w1.shape[2]
        head_dim = attn_wk.shape[1]
        window = k_cache.shape[1]
        chunk = width // n
        quarter = head_dim // 4
        freq = np.float64(ROPE_BASE) ** (-np.arange(quarter, dtype=np.float64) / quarter)
        invf = jnp.asarray(np.concatenate([freq, freq]).astype(np.float32)[None, :])
        exchange = [pltpu.VMEM((n, rows, chunk), BF16), pltpu.VMEM((n, rows, chunk), BF16), pltpu.VMEM((n, rows, chunk), BF16),
                    pltpu.SemaphoreType.DMA((2, n)), pltpu.SemaphoreType.DMA((2, n))]
        small = (x_in, norm_scale, conv_state, lru_state, rec_bx, rec_by, conv_w, conv_b, gate_ba, gate_bi, a_param, gate_wa, gate_wi,
                 rec_bout, mlp_b1, mlp_b2, mlp_bd, invf)
        big = (rec_wx, rec_wy, rec_wout, mlp_w1, mlp_w2, mlp_wd, attn_wq, attn_wk, attn_wv)
        row_out = jax.ShapeDtypeStruct((rows, chunk), BF16)
        head_out = jax.ShapeDtypeStruct((rows, head_dim), BF16)
        x_own, q, k_new, v_new, conv_new, lru_new = pl.pallas_call(
            functools.partial(first_kernel, n, layers),
            out_shape=(row_out, head_out, head_out, head_out,
                       jax.ShapeDtypeStruct(conv_state.shape, BF16), jax.ShapeDtypeStruct(lru_state.shape, F32)),
            in_specs=[SMEM] + [ANY] * (len(small) + len(big)),
            out_specs=(VMEM,) * 6,
            scratch_shapes=[vmem_like(a) for a in small] + [
                vmem_like(rec_wx), vmem_like(rec_wy), vmem_like(rec_wout),
                pltpu.VMEM((layers,) + mlp_w1.shape[1:], BF16), pltpu.VMEM((layers,) + mlp_w2.shape[1:], BF16),
                pltpu.VMEM((layers,) + mlp_wd.shape[1:], BF16), pltpu.VMEM((3,) + attn_wk.shape, BF16),
                pltpu.VMEM((rows, width), BF16), pltpu.VMEM((rows, hidden), BF16)] + exchange + [
                pltpu.SemaphoreType.DMA((len(small),)), pltpu.SemaphoreType.DMA((6 * layers + 3,))],
            compiler_params=pltpu.CompilerParams(collective_id=0, has_side_effects=True, vmem_limit_bytes=VMEM_LIMIT),
            name="recurrent_layers",
        )(tok_pos, *small, *big)

        heads, conv_out, lru_out, slot_out, k_out, v_out = pl.pallas_call(
            attend_kernel,
            out_shape=(head_out, jax.ShapeDtypeStruct(conv_state.shape, BF16), jax.ShapeDtypeStruct(lru_state.shape, F32),
                       jax.ShapeDtypeStruct(slot_pos.shape, jnp.int32), jax.ShapeDtypeStruct(k_cache.shape, BF16),
                       jax.ShapeDtypeStruct(v_cache.shape, BF16)),
            in_specs=[SMEM] + [VMEM] * 6 + [ANY] * 2,
            out_specs=(VMEM,) * 4 + (ANY,) * 2,
            scratch_shapes=[vmem_like(k_cache), vmem_like(v_cache), pltpu.VMEM((rows, window), F32), pltpu.SemaphoreType.DMA((2, 2, rows))],
            compiler_params=pltpu.CompilerParams(vmem_limit_bytes=VMEM_LIMIT),
            name="attend",
        )(tok_pos, q, k_new, v_new, conv_new, lru_new, slot_pos, k_cache, v_cache)

        tail = (heads, x_own, norm_scale, attn_bo[None, :], mlp_b1, mlp_b2, mlp_bd)
        x_out = pl.pallas_call(
            functools.partial(last_kernel, n, layers),
            out_shape=jax.ShapeDtypeStruct((rows, width), BF16),
            in_specs=[ANY] * (len(tail) + 4),
            out_specs=VMEM,
            scratch_shapes=[vmem_like(a) for a in tail] + [
                vmem_like(attn_wo), pltpu.VMEM(mlp_w1.shape[1:], BF16), pltpu.VMEM(mlp_w2.shape[1:], BF16), pltpu.VMEM(mlp_wd.shape[1:], BF16),
                pltpu.VMEM((rows, width), BF16), pltpu.VMEM((rows, hidden), BF16)] + exchange + [
                pltpu.SemaphoreType.DMA((len(tail),)), pltpu.SemaphoreType.DMA((4,))],
            compiler_params=pltpu.CompilerParams(collective_id=1, has_side_effects=True, vmem_limit_bytes=VMEM_LIMIT),
            name="last_mlp",
        )(*tail, attn_wo, mlp_w1, mlp_w2, mlp_wd)
        return (x_out, conv_out, lru_out, k_out, v_out, slot_out)

    return jax.shard_map(local_step, mesh=mesh, in_specs=in_specs, out_specs=out_specs, check_vma=False)
```

time: 765 us -> 130 us (0.17)
  waiting for transfers between devices: 625 us -> 0 us
  Pallas kernels: 0 us -> 123 us
  matrix products: 74.9 us -> 0 us
  other arithmetic: 48.2 us -> 0 us
  between operations: 14.5 us -> 0.66 us
    psum x6 -> x0, waiting for transfers between devices: 625 us -> none  [local_step(): lax.psum(part_sum.astype(jnp.bfloat16), 'tp')]
    pallas_call x0 -> x3, Pallas kernels: none -> 123 us  [the longest x1 67.6 us: local_step(): pl.pallas_call(functools.partial(first_kernel, n, layers), out_shape=(row...]
    dot_general x20 -> x0, matrix products: 74.9 us -> none  [the longest x3 23.2 us: mlp_update(): return jnp.dot(hidden, w_down, preferred_element_type=jnp.float32)]
    select_n x1 -> x0, other arithmetic: 28.5 us -> none  [write_cache(): k_next = jnp.where(target[:, :, None], k_new[:, None, :], k_cache)]
  transfers between devices with their start and end apart: 6 -> 0, of which waited for: 6 -> 0; matrix products, arithmetic and copies ran while one was open for 0% -> 0% of each run, Pallas kernels for 0% -> 0%
where the time goes in v1:
time: 130 us
  Pallas kernels  123 us (95%)
  local copies, waits for them, and re-layouts  5.8 us (4%)
    pallas_call x1, Pallas kernels, local_step(): pl.pallas_call(functools.partial(first_kernel, n, layers), out_shape=(row...  67.6 us
    pallas_call x1, Pallas kernels, local_step(): pl.pallas_call(functools.partial(last_kernel, n, layers), out_shape=jax.S...  30.5 us
    pallas_call x1, Pallas kernels, local_step(): pl.pallas_call(attend_kernel, out_shape=(head_out, jax.ShapeDtypeStruct(c...  25.2 us
    unnamed x3, local copies, waits for them, and re-layouts  4.5 us

profile of v1, /device:TPU:21, one launch (start us, length us, event | category | flops | bytes accessed | tf_op | source)
XLA Modules:
  0.0 129.7 jit_solution(9139497742443144059)
XLA Ops:
  0.6 1.3 %broadcast_in_dim.3.refs_3_ = bf16[1,4096]{1,0:T(2,128)(2,1)} reshape(bf16[4096]{0:T(1024)(128)(2,1)} %param.58) | data formatting | bytes 16384 | tf_op jit(solution)/shard_map/broadcast_in_dim | solution.py:374
  1.9 1.5 %copy.39.refs_2_ = bf16[2,16,3,256]{3,2,1,0:T(4,128)(2,1)} copy(bf16[2,16,3,256]{3,1,2,0:T(8,128)(2,1)} %param.35) | data formatting | bytes 98304 | tf_op args[2]
  3.4 67.6 %recurrent_layers.1 = (bf16[16,256]{1,0:T(8,128)(2,1)}, bf16[16,256]{1,0:T(8,128)(2,1)}, bf16[16,256]{1,0:T(8,128)(2,1)}, bf16[16,256]{1,0:T(8,128)(2,1)}, bf16[...) custom-call(s32[16]{0:T(128)} %pos_ref.3, bf16[16,4096]{1,0:T(8,128)(2,1)} %refs_0_.1, bf16[3,2,4096]{2,1,0:T(2,128)(2,1)} %refs_2_.2, ...), custom_call_target="tpu_custom_call" | custom-call | tf_op jit(solution)/shard_map/recurrent_layers/pallas_call | solution.py:346
  71.0 25.2 %attend.1 = (bf16[16,256]{1,0:T(8,128)(2,1)}, bf16[2,16,3,256]{3,2,1,0:T(4,128)(2,1)}, f32[2,16,256]{2,1,0:T(8,128)}, s32[16,2048]{1,0:T(8,128)}, bf16[16,2048,2...) custom-call(s32[16]{0:T(128)} %pos_ref.3, bf16[16,256]{1,0:T(8,128)(2,1)} %get-tuple-element.18.q_ref, ...), custom_call_target="tpu_custom_call" | custom-call | tf_op jit(solution)/shard_map/attend/pallas_call | solution.py:362
  96.1 1.5 %copy.40 = bf16[2,16,3,256]{3,1,2,0:T(8,128)(2,1)} copy(bf16[2,16,3,256]{3,2,1,0:T(4,128)(2,1)} %get-tuple-element.31) | data formatting | bytes 98304
  97.6 30.5 %last_mlp.1 = bf16[16,4096]{1,0:T(8,128)(2,1)} custom-call(bf16[16,256]{1,0:T(8,128)(2,1)} %get-tuple-element.23.refs_0_, bf16[16,256]{1,0:T(8,128)(2,1)} %get-tuple-element.24.refs_1_, bf16[3,2,4096]{2,1,0:T(2,128)(2,1)} %refs_2_.2, bf16[1,4096]{1,0:T(2,128)(2,1)} %broadcast_in_dim.3.refs_3_, bf16[3,768]{1,0:T(4,128)(2,1)} %refs_4_.3, ...), custom_call_target="tpu_custom_call" | custom-call | tf_op jit(solution)/shard_map/last_mlp/pallas_call | solution.py:375
  128.2 1.6 %copy.42 = bf16[16,4096]{1,0:T(8,128)(2,1)} copy(bf16[16,4096]{1,0:T(8,128)(2,1)} %last_mlp.1) | data formatting | bytes 262144
